TPU v7x, 32 devices: a whole 2x2x4 slice. The times are simulated.
32 devices in a mesh: groups: 2 (over x), dom: 16 (over z, y, core).
Axes of the slice: x: 2, y: 2, z: 4, core: 2. Of those that a mesh axis runs over, the one named last changes fastest.
Arguments:
- node_latent: bfloat16 [32768, 128], P(('groups', 'dom')), parts along dimension 0, may hold values from -6 to 6
- edge_latent: bfloat16 [196608, 128], P(('groups', 'dom')), parts along dimension 0, may hold values from -6 to 6
- node_cot: bfloat16 [32768, 128], P(('groups', 'dom')), parts along dimension 0, may hold values from -6 to 6
- edge_cot: bfloat16 [196608, 128], P(('groups', 'dom')), parts along dimension 0, may hold values from -6 to 6
- base_pos: float32 [3, 32768], P(None, ('groups', 'dom')), parts along dimension 1
- centers: float32 [3, 2048], replicated, may hold values from 0 to 1
- amplitudes: float32 [3, 2048], replicated, may hold values from -0.3 to 0.3
- edge_in: bfloat16 [384, 128], replicated, may hold values from -0.3125 to 0.3125
- edge_geo: float32 [4, 128], replicated, may hold values from -3 to 3
- edge_out: bfloat16 [128, 128], replicated, may hold values from -0.5 to 0.5
- edge_gain: float32 [128], replicated, may hold values from 0.5 to 1.5
- node_in: bfloat16 [256, 128], replicated, may hold values from -0.375 to 0.375
- node_out: bfloat16 [128, 128], replicated, may hold values from -0.5 to 0.5
- node_gain: float32 [128], replicated, may hold values from 0.5 to 1.5
- senders: int32 [196608], P(('groups', 'dom')), parts along dimension 0, may hold values from 0 to 3071, as said below
- receivers: int32 [196608], P(('groups', 'dom')), parts along dimension 0, may hold values from 0 to 1023
- send_rows: int32 [32, 16, 128], P(('groups', 'dom')), parts along dimension 0, may hold values from 0 to 1023
Outputs:
- grad_nodes: float32 [32768, 128], P(('groups', 'dom')), parts along dimension 0
- grad_edges: float32 [196608, 128], P(('groups', 'dom')), parts along dimension 0
- grad_controls: float32 [6, 2048], P('groups'), parts along dimension 0
There are 2 independent parts, one for each index of `groups`. A program takes and returns all parts, laid end to end along the dimension named above; an argument that names none is the same for every part. Nothing has to cross between parts.
Inputs may be any that keep to these rules, and one draw needn't show every extreme that they name: `senders`: for edge j in partition q = j // 6144: a value below 1024 is an own node; a value v of 1024 or more names slot (v - 1024) % 128 of the block from partition p = (v - 1024) // 128, and 1 <= |p - q| <= 2. Every partition has an edge using slot 127 of some block.
All inputs are finite; a program needn't handle non-finite values.
Results may differ from a plain program's by a relative error of at most 0.0085.
Values may be sent and summed in bfloat16 or wider, within the bound.
A program may use at most 128 MiB of HBM per device.

v0:
```python
import functools

import jax
import jax.numpy as jnp
from jax import lax
from jax.experimental import pallas as pl
from jax.experimental.pallas import tpu as pltpu
from jax.sharding import PartitionSpec as P

REACH = 2
RBF_RATE = 78.125
OFFSETS = [step for step in range(-REACH, REACH + 1) if step != 0]
NEAR = len(OFFSETS)
F32 = jnp.float32
BF16 = jnp.bfloat16
VMEM_FULL = pl.BlockSpec(memory_space=pltpu.VMEM)


def dot(a, b):
    return jnp.dot(a, b, preferred_element_type=F32)


def dot_t(a, b):
    return lax.dot_general(a, b, (((1,), (1,)), ((), ())), preferred_element_type=F32)


def stack_rows(rows, height):
    at = lax.broadcasted_iota(jnp.int32, (height, rows[0].shape[1]), 0)
    out = jnp.zeros(at.shape, F32)
    for k, row in enumerate(rows):
        out = jnp.where(at == k, row, out)
    return out


def split(x):
    hi = x.astype(BF16)
    return hi, (x - hi.astype(F32)).astype(BF16)


def columns_match(row, width):
    block = row.shape[1]
    group = row // 128
    within = (row - group * 128).astype(F32)
    within = jnp.transpose(jnp.broadcast_to(within, (128, block)))
    group = jnp.transpose(jnp.broadcast_to(group.astype(F32), (128, block)))
    lane = lax.broadcasted_iota(jnp.int32, (block, 128), 1).astype(F32)
    key = jnp.where(within == lane, group, -1.0).astype(BF16)
    one, zero = jnp.ones_like(key), jnp.zeros_like(key)
    return jnp.concatenate(
        [jnp.where(key == jnp.full_like(key, j), one, zero) for j in range(width // 128)], axis=1
    )


def rows_match(row, height, first=0):
    block = row.shape[1]
    group = row // 16
    at = lax.broadcasted_iota(jnp.int32, (16, block), 0)
    key = jnp.where(at == row - group * 16, group, -1).astype(F32).astype(BF16)
    one, zero = jnp.ones_like(key), jnp.zeros_like(key)
    return jnp.concatenate(
        [
            jnp.where(key == jnp.full_like(key, q), one, zero)
            for q in range(first // 16, (first + height) // 16)
        ],
        axis=0,
    )


def lanes_like(x):
    return lax.broadcasted_iota(jnp.int32, x.shape, 1)


def prepare_kernel(lat_ref, pos_ref, cen_ref, amp_ref, rows_ref, table_ref, out_ref, amp_s):
    step = pl.program_id(0)
    block = lat_ref.shape[0]

    @pl.when(step == 0)
    def _():
        hi, lo = split(amp_ref[...])
        hi, lo = hi.astype(F32), lo.astype(F32)
        rows = [hi[k : k + 1] for k in range(3)]
        zero = jnp.zeros_like(rows[0])
        rows = rows + [zero] + [lo[k : k + 1] for k in range(3)]
        amp_s[...] = stack_rows(rows, 128).astype(BF16)

    base = jnp.transpose(stack_rows([pos_ref[k : k + 1, :] for k in range(3)], 128))
    squared = None
    for k in range(3):
        off = base[:, k : k + 1] - cen_ref[k : k + 1, :]
        squared = off * off if squared is None else squared + off * off
    phi_hi, phi_lo = split(jnp.exp(-RBF_RATE * squared))
    moved = dot_t(phi_hi, amp_s[...]) + dot_t(phi_lo, amp_s[...])
    moved = moved + pltpu.roll(moved, 124, 1)
    lane = lanes_like(base)
    placed = jnp.where(lane < 3, base + moved, 0.0)
    hi = placed.astype(BF16).astype(F32)
    rest = placed - hi
    mid = rest.astype(BF16).astype(F32)
    low = (rest - mid).astype(BF16).astype(F32)
    parts = hi + pltpu.roll(mid, 4, 1) + pltpu.roll(low, 8, 1)
    at = pl.ds(pl.multiple_of(step * block, block), block)
    width = lat_ref.shape[1]
    table_ref[at, :width] = lat_ref[...]
    table_ref[at, width:] = parts.astype(BF16)

    @pl.when(step == pl.num_programs(0) - 1)
    def _():
        match = columns_match(rows_ref[...], table_ref.shape[0])
        out_ref[...] = dot(match, table_ref[...]).astype(BF16)


def prepare(node_latent, base_pos, centers, amplitudes, rows):
    nodes, width = node_latent.shape
    block = 256
    count = rows.shape[1]
    full = lambda shape: pl.BlockSpec(shape, lambda i: (0,) * len(shape))
    return pl.pallas_call(
        prepare_kernel,
        grid=(nodes // block,),
        in_specs=[
            pl.BlockSpec((block, width), lambda i: (i, 0)),
            pl.BlockSpec((3, block), lambda i: (0, i)),
            full(centers.shape),
            full(amplitudes.shape),
            full(rows.shape),
        ],
        out_specs=[full((nodes, width + 128)), full((count, width + 128))],
        out_shape=[
            jax.ShapeDtypeStruct((nodes, width + 128), BF16),
            jax.ShapeDtypeStruct((count, width + 128), BF16),
        ],
        scratch_shapes=[pltpu.VMEM((128, centers.shape[1]), BF16)],
        compiler_params=pltpu.CompilerParams(dimension_semantics=("arbitrary",)),
        name="prepare",
    )(node_latent, base_pos, centers, amplitudes, rows)


def exchange_kernel(parts, x_ref, o_ref, send_sem, recv_sem):
    me = lax.axis_index("dom")
    partners = [lax.rem(me + off + parts, parts) for off in OFFSETS]
    barrier = pltpu.get_barrier_semaphore()
    for partner in partners:
        pl.semaphore_signal(
            barrier, inc=1, device_id={"dom": partner}, device_id_type=pl.DeviceIdType.MESH
        )
    pl.semaphore_wait(barrier, NEAR)
    copies = []
    for k, partner in enumerate(partners):
        there = NEAR - 1 - k
        copy = pltpu.make_async_remote_copy(
            src_ref=x_ref.at[k],
            dst_ref=o_ref.at[there],
            send_sem=send_sem.at[k],
            recv_sem=recv_sem.at[there],
            device_id={"dom": partner},
            device_id_type=pl.DeviceIdType.MESH,
        )
        copy.start()
        copies.append(copy)
    for copy in copies:
        copy.wait()


def exchange(blocks, parts, ident):
    return pl.pallas_call(
        functools.partial(exchange_kernel, parts),
        out_shape=jax.ShapeDtypeStruct(blocks.shape, blocks.dtype),
        in_specs=[VMEM_FULL],
        out_specs=VMEM_FULL,
        scratch_shapes=[pltpu.SemaphoreType.DMA((NEAR,)), pltpu.SemaphoreType.DMA((NEAR,))],
        compiler_params=pltpu.CompilerParams(collective_id=ident, has_side_effects=True),
        name=f"exchange_{ident}",
    )(blocks)


def total_kernel(parts, x_ref, o_ref, work, got, send_sem, recv_sem):
    steps = parts.bit_length() - 1
    me = lax.axis_index("dom")
    partners = []
    for s in range(steps):
        bit = lax.rem(me // (1 << s), 2)
        partners.append(me + (1 << s) * (1 - 2 * bit))
    barrier = pltpu.get_barrier_semaphore()
    for partner in partners:
        pl.semaphore_signal(
            barrier, inc=1, device_id={"dom": partner}, device_id_type=pl.DeviceIdType.MESH
        )
    pl.semaphore_wait(barrier, steps)
    for s, partner in enumerate(partners):
        source = x_ref if s == 0 else work.at[s - 1]
        copy = pltpu.make_async_remote_copy(
            src_ref=source,
            dst_ref=got.at[s],
            send_sem=send_sem.at[s],
            recv_sem=recv_sem.at[s],
            device_id={"dom": partner},
            device_id_type=pl.DeviceIdType.MESH,
        )
        copy.start()
        copy.wait()
        target = o_ref if s == steps - 1 else work.at[s]
        target[...] = source[...] + got[s]


def total(values, parts, ident):
    steps = parts.bit_length() - 1
    if parts != 1 << steps or steps == 0:
        return lax.psum(values, "dom")
    return pl.pallas_call(
        functools.partial(total_kernel, parts),
        out_shape=jax.ShapeDtypeStruct(values.shape, values.dtype),
        in_specs=[VMEM_FULL],
        out_specs=VMEM_FULL,
        scratch_shapes=[
            pltpu.VMEM((steps,) + values.shape, values.dtype),
            pltpu.VMEM((steps,) + values.shape, values.dtype),
            pltpu.SemaphoreType.DMA((steps,)),
            pltpu.SemaphoreType.DMA((steps,)),
        ],
        compiler_params=pltpu.CompilerParams(collective_id=ident, has_side_effects=True),
        name="total",
    )(values)


def normed_of(values):
    centred = values - jnp.mean(values, axis=-1, keepdims=True)
    inv = lax.rsqrt(jnp.mean(centred * centred, axis=-1, keepdims=True) + 1e-05)
    return centred * inv, inv


def norm_back(values, gain, upstream):
    normed, inv = normed_of(values)
    scaled = upstream * gain
    return inv * (
        scaled
        - jnp.mean(scaled, axis=-1, keepdims=True)
        - normed * jnp.mean(scaled * normed, axis=-1, keepdims=True)
    )


def silu_slope(values):
    sigma = jax.nn.sigmoid(values)
    return sigma * (1.0 + values * (1.0 - sigma))


def edges_kernel(
    sidx_ref,
    ridx_ref,
    table_ref,
    halo_ref,
    elat_ref,
    ecot_ref,
    ncot_ref,
    ein_ref,
    egeo_ref,
    eout_ref,
    egain_ref,
    nin_ref,
    nout_ref,
    ngain_ref,
    gedge_ref,
    gnode_ref,
    gpos_ref,
    back_ref,
    pre_s,
    mid_s,
    geo_s,
    agg_s,
    gagg_s,
    geo_rows,
    geo_cols,
    own_s,
    away_s,
    recv_s,
):
    phase = pl.program_id(0)
    step = pl.program_id(1)
    last = pl.num_programs(1) - 1
    nodes = table_ref.shape[0]
    block, width = elat_ref.shape
    away = halo_ref.shape[0]
    at = pl.ds(pl.multiple_of(step * block, block), block)
    srow = sidx_ref[0]
    rrow = ridx_ref[0]

    @pl.when((phase == 0) & (step == 0))
    def _():
        agg_s[...] = jnp.zeros_like(agg_s)
        own_s[...] = jnp.zeros_like(own_s)
        away_s[...] = jnp.zeros_like(away_s)
        recv_s[...] = jnp.zeros_like(recv_s)
        hi, lo = split(stack_rows([egeo_ref[k : k + 1, :] for k in range(4)], 128))
        geo_rows[...] = jnp.concatenate([hi, hi, lo], axis=0)
        geo_cols[...] = jnp.concatenate([hi, hi, lo], axis=1)

    @pl.when(phase == 0)
    def _():
        match = columns_match(srow, nodes + away)
        sent = dot(match[:, :nodes], table_ref[...]) + dot(match[:, nodes:], halo_ref[...])
        got = dot(columns_match(rrow, nodes), table_ref[...])
        apart = sent[:, width:] - got[:, width:]
        delta = apart + (pltpu.roll(apart, 124, 1) + pltpu.roll(apart, 120, 1))
        lane = lanes_like(delta)
        delta = jnp.where(lane < 3, delta, 0.0)
        length = jnp.sqrt(jnp.sum(delta * delta, axis=-1, keepdims=True) + 0.01)
        geo = jnp.where(lane == 3, length, delta)
        geo_hi, geo_lo = split(geo)
        latent = elat_ref[...]
        joined = jnp.concatenate(
            [sent[:, :width].astype(BF16), got[:, :width].astype(BF16), latent], axis=1
        )
        pre = dot(joined, ein_ref[...]) + dot(
            jnp.concatenate([geo_hi, geo_lo, geo_hi], axis=1), geo_rows[...]
        )
        hidden = (pre * jax.nn.sigmoid(pre)).astype(BF16)
        mid = dot(hidden, eout_ref[...])
        normed, _ = normed_of(mid)
        updated = (latent.astype(F32) + normed * egain_ref[...]).astype(BF16)
        agg_s[...] += dot(rows_match(rrow, nodes), updated)
        pre_s[at, :] = pre
        mid_s[at, :] = mid
        geo_s[at, :] = geo

    @pl.when((phase == 0) & (step == last))
    def _():
        latent = table_ref[:, :width]
        w_node = nin_ref[:width, :]
        w_agg = nin_ref[width:, :]
        cot = ncot_ref[...].astype(F32)
        node_pre = dot(latent, w_node) + dot(agg_s[...].astype(BF16), w_agg)
        node_hidden = (node_pre * jax.nn.sigmoid(node_pre)).astype(BF16)
        node_mid = dot(node_hidden, nout_ref[...])
        grad_mid = norm_back(node_mid, ngain_ref[...], cot).astype(BF16)
        grad_pre = (dot_t(grad_mid, nout_ref[...]) * silu_slope(node_pre)).astype(BF16)
        gagg_s[...] = dot_t(grad_pre, w_agg).astype(BF16)
        agg_s[...] = cot + dot_t(grad_pre, w_node)

    @pl.when(phase == 1)
    def _():
        pre = pre_s[at, :]
        mid = mid_s[at, :]
        geo = geo_s[at, :]
        grad_upd = ecot_ref[...].astype(F32) + dot(columns_match(rrow, nodes), gagg_s[...])
        grad_mid = norm_back(mid, egain_ref[...], grad_upd).astype(BF16)
        grad_pre = dot_t(grad_mid, eout_ref[...]) * silu_slope(pre)
        hi, lo = split(grad_pre)
        back = dot_t(hi, ein_ref[...])
        gedge_ref[...] = grad_upd + back[:, 2 * width :]
        grad_geo = dot_t(jnp.concatenate([hi, lo, hi], axis=1), geo_cols[...])
        lane = lanes_like(geo)
        pick = lane == 3
        ratio = jnp.sum(jnp.where(pick, grad_geo, 0.0), axis=-1, keepdims=True) / jnp.sum(
            jnp.where(pick, geo, 0.0), axis=-1, keepdims=True
        )
        grad_delta = jnp.where(lane < 3, grad_geo + geo * ratio, 0.0)
        d_hi, d_lo = split(grad_delta)
        parts = (d_hi.astype(F32) + pltpu.roll(d_lo.astype(F32), 4, 1)).astype(BF16)
        to_send = jnp.concatenate([back[:, :width].astype(BF16), parts], axis=1)
        to_recv = jnp.concatenate([back[:, width : 2 * width].astype(BF16), parts], axis=1)
        own_s[...] += dot(rows_match(srow, nodes), to_send)
        away_s[...] += dot(rows_match(srow, away, nodes), to_send)
        recv_s[...] += dot(rows_match(rrow, nodes), to_recv)

    @pl.when((phase == 1) & (step == last))
    def _():
        gnode_ref[...] = agg_s[...] + own_s[:, :width] + recv_s[:, :width]
        moved = own_s[:, width:] - recv_s[:, width:]
        moved = moved + pltpu.roll(moved, 124, 1)
        gpos_ref[...] = jnp.where(lanes_like(moved) < 3, moved, 0.0)
        there = away_s[:, width:]
        there = there + pltpu.roll(there, 124, 1)
        there = jnp.where(lanes_like(there) < 3, there, 0.0)
        hi, lo = split(there)
        back_ref[:, :width] = away_s[:, :width].astype(BF16)
        back_ref[:, width:] = (hi.astype(F32) + pltpu.roll(lo.astype(F32), 4, 1)).astype(BF16)


def edges(senders, receivers, table, halo, edge_latent, edge_cot, node_cot, weights):
    block = 1024 if edge_latent.shape[0] % 1024 == 0 else 512
    count, width = edge_latent.shape
    turns = count // block
    nodes = table.shape[0]
    away = halo.shape[0]
    wide = table.shape[1]
    full = lambda shape: pl.BlockSpec(shape, lambda p, i: (0,) * len(shape))
    index_spec = pl.BlockSpec((1, 1, block), lambda p, i: (i, 0, 0))
    second = pl.BlockSpec((block, width), lambda p, i: (i * p, 0))
    return pl.pallas_call(
        edges_kernel,
        grid=(2, turns),
        in_specs=[
            index_spec,
            index_spec,
            full(table.shape),
            full(halo.shape),
            pl.BlockSpec((block, width), lambda p, i: (i * (1 - p), 0)),
            second,
            full(node_cot.shape),
        ]
        + [full(w.shape) for w in weights],
        out_specs=[second, full((nodes, width)), full((nodes, 128)), full((away, wide))],
        out_shape=[
            jax.ShapeDtypeStruct((count, width), F32),
            jax.ShapeDtypeStruct((nodes, width), F32),
            jax.ShapeDtypeStruct((nodes, 128), F32),
            jax.ShapeDtypeStruct((away, wide), BF16),
        ],
        scratch_shapes=[
            pltpu.VMEM((count, width), F32),
            pltpu.VMEM((count, width), F32),
            pltpu.VMEM((count, 128), F32),
            pltpu.VMEM((nodes, width), F32),
            pltpu.VMEM((nodes, width), BF16),
            pltpu.VMEM((384, width), BF16),
            pltpu.VMEM((128, 3 * width), BF16),
            pltpu.VMEM((nodes, wide), F32),
            pltpu.VMEM((away, wide), F32),
            pltpu.VMEM((nodes, wide), F32),
        ],
        compiler_params=pltpu.CompilerParams(
            dimension_semantics=("arbitrary", "arbitrary"), vmem_limit_bytes=58 * 1024 * 1024
        ),
        name="edges",
    )(
        senders.reshape(turns, 1, block),
        receivers.reshape(turns, 1, block),
        table,
        halo,
        edge_latent,
        edge_cot,
        node_cot,
        *weights,
    )


def finish_kernel(rows_ref, got_ref, gnode_ref, gpos_ref, pos_ref, cen_ref, out_ref, amp_ref, gp_s):
    width = gnode_ref.shape[1]

    @pl.when(pl.program_id(0) == 0)
    def _():
        back = dot(rows_match(rows_ref[...], gnode_ref.shape[0]), got_ref[...])
        out_ref[...] = gnode_ref[...] + back[:, :width]
        moved = back[:, width:]
        moved = gpos_ref[...] + (moved + pltpu.roll(moved, 124, 1))
        moved = jnp.where(lanes_like(moved) < 3, moved, 0.0)
        hi, lo = split(moved)
        gp_s[...] = (hi.astype(F32) + pltpu.roll(lo.astype(F32), 4, 1)).astype(BF16)

    cen = jnp.transpose(stack_rows([cen_ref[k : k + 1, :] for k in range(3)], 128))
    squared = None
    for k in range(3):
        off = pos_ref[k : k + 1, :] - cen[:, k : k + 1]
        squared = off * off if squared is None else squared + off * off
    phi_hi, phi_lo = split(jnp.exp(-RBF_RATE * squared))
    amp = dot(phi_hi, gp_s[...]) + dot(phi_lo, gp_s[...])
    amp = amp + pltpu.roll(amp, 124, 1)
    amp_ref[...] = jnp.transpose(amp)[:8, :]


def finish(rows, got, gnode, gpos, base_pos, centers):
    nodes, width = gnode.shape
    controls = centers.shape[1]
    block = 512
    full = lambda shape: pl.BlockSpec(shape, lambda i: (0,) * len(shape))
    return pl.pallas_call(
        finish_kernel,
        grid=(controls // block,),
        in_specs=[
            full(rows.shape),
            full(got.shape),
            full(gnode.shape),
            full(gpos.shape),
            full(base_pos.shape),
            pl.BlockSpec((3, block), lambda i: (0, i)),
        ],
        out_specs=[full(gnode.shape), pl.BlockSpec((8, block), lambda i: (0, i))],
        out_shape=[
            jax.ShapeDtypeStruct(gnode.shape, F32),
            jax.ShapeDtypeStruct((8, controls), F32),
        ],
        scratch_shapes=[pltpu.VMEM((nodes, 128), BF16)],
        compiler_params=pltpu.CompilerParams(dimension_semantics=("arbitrary",)),
        name="finish",
    )(rows, got, gnode, gpos, base_pos, centers)


def shards(
    node_latent,
    edge_latent,
    node_cot,
    edge_cot,
    base_pos,
    centers,
    amplitudes,
    edge_in,
    edge_geo,
    edge_out,
    edge_gain,
    node_in,
    node_out,
    node_gain,
    senders,
    receivers,
    send_rows,
):
    nodes = node_latent.shape[0]
    parts = lax.axis_size("dom")
    slots = send_rows.shape[2]
    me = lax.axis_index("dom")
    slot = jnp.maximum(senders - nodes, 0)
    off = slot // slots - me
    near = jnp.clip(jnp.where(off < 0, off + REACH, off + REACH - 1), 0, NEAR - 1)
    compact = jnp.where(senders >= nodes, nodes + near * slots + slot % slots, senders)
    twice = jnp.concatenate([send_rows[0], send_rows[0]], 0)
    around = lax.dynamic_slice_in_dim(twice, (me + parts - REACH) % parts, 2 * REACH + 1, 0)
    rows = jnp.concatenate([around[:REACH], around[REACH + 1 :]], 0).reshape(1, NEAR * slots)
    table, out = prepare(node_latent, base_pos, centers, amplitudes, rows)
    wide = table.shape[1]
    halo = exchange(out.reshape(NEAR, slots, wide), parts, 0).reshape(NEAR * slots, wide)
    weights = (
        edge_in,
        edge_geo,
        edge_out,
        edge_gain[None, :],
        node_in,
        node_out,
        node_gain[None, :],
    )
    grad_edges, gnode, gpos, back = edges(
        compact, receivers, table, halo, edge_latent, edge_cot, node_cot, weights
    )
    got = exchange(back.reshape(NEAR, slots, wide), parts, 1).reshape(NEAR * slots, wide)
    grad_nodes, amp = finish(rows, got, gnode, gpos, base_pos, centers)
    grad_controls = total(amp, parts, 2)[:3]
    return (grad_nodes, grad_edges, grad_controls)


def solution(mesh):
    split_rows = P(("groups", "dom"), None)
    in_specs = (
        split_rows,
        split_rows,
        split_rows,
        split_rows,
        P(None, ("groups", "dom")),
        P(),
        P(),
        P(),
        P(),
        P(),
        P(),
        P(),
        P(),
        P(),
        P(("groups", "dom")),
        P(("groups", "dom")),
        P(("groups", "dom"), None, None),
    )
    out_specs = (split_rows, split_rows, P("groups", None))
    return jax.shard_map(shards, mesh=mesh, in_specs=in_specs, out_specs=out_specs, check_vma=False)
```

profile of v0, /device:TPU:0, one launch (start us, length us, event | category | flops | bytes accessed | tf_op | source)
XLA Modules:
  0.0 111.2 jit_solution(9925265579794482111)
XLA Ops:
  0.6 0.7 fusion.3
  1.4 0.6 pad_add_fusion
  2.0 1.4 %compare_select_fusion = s32[6144]{0:T(1024)} fusion(s32[6144]{0:T(1024)} %param.31, s32[]{:T(128)S(6)} %axis_index.12), kind=kLoop, calls=%fused_computation | loop fusion | flops 153600 | bytes 49156 | tf_op jit(solution)/shard_map/jit(_where)/select_n | solution.py:513
  3.4 7.9 %prepare.1 = (bf16[1024,256]{1,0:T(8,128)(2,1)}, bf16[512,256]{1,0:T(8,128)(2,1)}) custom-call(bf16[1024,128]{1,0:T(8,128)(2,1)} %lat_ref.1, f32[3,1024]{1,0:T(4,128)} %pos_ref.3, f32[3,2048]{1,0:T(4,128)} %cen_ref.3, f32[3,2048]{1,0:T(4,128)} %amp_ref.1, s32[1,512]{1,0:T(1,128)} %bitcast.16), custom_call_target="tpu_custom_call" | custom-call | tf_op jit(solution)/shard_map/prepare/pallas_call | solution.py:117
  11.3 11.3 %exchange_0.1 = bf16[4,128,256]{2,1,0:T(8,128)(2,1)} custom-call(bf16[4,128,256]{2,1,0:T(8,128)(2,1)} %bitcast.13), custom_call_target="tpu_custom_call" | custom-call | tf_op jit(solution)/shard_map/exchange_0/pallas_call | solution.py:165
  22.6 54.8 %edges.1 = (f32[6144,128]{1,0:T(8,128)}, f32[1024,128]{1,0:T(8,128)}, f32[1024,128]{1,0:T(8,128)}, bf16[512,256]{1,0:T(8,128)(2,1)}) custom-call(s32[6,1,1024]{2,1,0:T(1,128)} %bitcast.14, s32[6,1,1024]{2,1,0:T(1,128)} %bitcast.15, bf16[1024,256]{1,0:T(8,128)(2,1)} %get-tuple-element.11.table_ref, bf16[512,256]{1,0:T(8,128)(2,1)} %bitcast.10, ...), custom_call_target="tpu_custom_call" | custom-call | tf_op jit(solution)/shard_map/edges/pallas_call | solution.py:388
  77.4 9.4 %exchange_1.1 = bf16[4,128,256]{2,1,0:T(8,128)(2,1)} custom-call(bf16[4,128,256]{2,1,0:T(8,128)(2,1)} %bitcast.12), custom_call_target="tpu_custom_call" | custom-call | tf_op jit(solution)/shard_map/exchange_1/pallas_call | solution.py:165
  86.8 8.5 %finish.1 = (f32[1024,128]{1,0:T(8,128)}, f32[8,2048]{1,0:T(8,128)}) custom-call(s32[1,512]{1,0:T(1,128)} %bitcast.17, bf16[512,256]{1,0:T(8,128)(2,1)} %bitcast.11, f32[1024,128]{1,0:T(8,128)} %get-tuple-element.14.gnode_ref, f32[1024,128]{1,0:T(8,128)} %get-tuple-element.15.gpos_ref, f32[3,1024]{1,0:T(4,128)} %pos_ref.3, f32[3,2048]{1,0:T(4,128)} %cen_ref.3), custom_call_target="tpu_custom_call" | custom-call | tf_op jit(solution)/shard_map/finish/pallas_call | solution.py:465
  95.2 14.5 %total.1 = f32[8,2048]{1,0:T(8,128)} custom-call(f32[8,2048]{1,0:T(8,128)} %get-tuple-element.18.x_ref), custom_call_target="tpu_custom_call" | custom-call | tf_op jit(solution)/shard_map/total/pallas_call | solution.py:209
  109.7 1.5 %slice.11 = f32[3,2048]{1,0:T(4,128)} slice(f32[8,2048]{1,0:T(8,128)} %total.1), slice={[0:3], [0:2048]} | slice | bytes 49152 | tf_op jit(solution)/shard_map/slice | solution.py:534
  (1 shorter events, 0.0 us)
where the time goes:
time: 112 us; the launch traced here: 111 us
  Pallas kernels  106 us (95%)
  other arithmetic  2.7 us (2%)
  local copies, waits for them, and re-layouts  1.47 us (1%)
    pallas_call x1, Pallas kernels, edges(): pl.pallas_call(edges_kernel, grid=(2, turns), in_specs=[index_spec, index...  54.8 us
    pallas_call x2, Pallas kernels, exchange(): pl.pallas_call(functools.partial(exchange_kernel, parts), out_shape=jax.S...  20.7 us
    pallas_call x1, Pallas kernels, total(): pl.pallas_call(functools.partial(total_kernel, parts), out_shape=jax.Shap...  14.5 us
    pallas_call x1, Pallas kernels, finish(): pl.pallas_call(finish_kernel, grid=(controls // block,), in_specs=[full(r...  8.46 us
    pallas_call x1, Pallas kernels, prepare(): pl.pallas_call(prepare_kernel, grid=(nodes // block,), in_specs=[pl.Block...  7.94 us

commit v1 on v0

v1 whole, which is shorter than its diff:
```python
import functools

import jax
import jax.numpy as jnp
from jax import lax
from jax.experimental import pallas as pl
from jax.experimental.pallas import tpu as pltpu
from jax.sharding import PartitionSpec as P

REACH = 2
RBF_RATE = 78.125
SCALE = (RBF_RATE * 1.4426950408889634) ** 0.5
FAR = 4.0 * SCALE
OFFSETS = [step for step in range(-REACH, REACH + 1) if step != 0]
NEAR = len(OFFSETS)
F32 = jnp.float32
BF16 = jnp.bfloat16
LANES = 128
VMEM_FULL = pl.BlockSpec(memory_space=pltpu.VMEM)
ANY = pl.BlockSpec(memory_space=pl.ANY)


def dot(a, b):
    return jnp.dot(a, b, preferred_element_type=F32)


def dot_t(a, b):
    return lax.dot_general(a, b, (((1,), (1,)), ((), ())), preferred_element_type=F32)


def stack_rows(rows, height):
    at = lax.broadcasted_iota(jnp.int32, (height, rows[0].shape[1]), 0)
    out = jnp.zeros(at.shape, F32)
    for k, row in enumerate(rows):
        if row is not None:
            out = jnp.where(at == k, row, out)
    return out


def split(x):
    hi = x.astype(BF16)
    return hi, (x - hi.astype(F32)).astype(BF16)


def three(x):
    hi = x.astype(BF16).astype(F32)
    rest = x - hi
    mid = rest.astype(BF16).astype(F32)
    return hi, mid, rest - mid


def as_columns(row):
    wide = jnp.broadcast_to(row.astype(F32), (LANES, row.shape[1])).astype(BF16)
    return jnp.transpose(wide)


def lane_iota(shape):
    return lax.broadcasted_iota(jnp.int32, shape, 1).astype(F32).astype(BF16)


def tiles_match(key, count):
    one, zero = jnp.ones_like(key), jnp.zeros_like(key)
    return jnp.concatenate(
        [jnp.where(key == jnp.full_like(key, j), one, zero) for j in range(count)], axis=1
    )


def columns_match(row, width):
    within = as_columns(row % LANES)
    tile = as_columns(row // LANES)
    key = jnp.where(within == lane_iota(within.shape), tile, jnp.full_like(tile, -1.0))
    return tiles_match(key, width // LANES)


def rows_match(row, height):
    block = row.shape[1]
    group = row // 16
    at = lax.broadcasted_iota(jnp.int32, (16, block), 0)
    key = jnp.where(at == row - group * 16, group, -1).astype(F32).astype(BF16)
    one, zero = jnp.ones_like(key), jnp.zeros_like(key)
    return jnp.concatenate(
        [jnp.where(key == jnp.full_like(key, q), one, zero) for q in range(height // 16)], axis=0
    )


def lane_gather(table_ref, row, count):
    block = row.shape[1]
    lane = jnp.broadcast_to(row % LANES, (8, block))
    tile = jnp.broadcast_to(row // LANES, (8, block))
    pieces = []
    for j in range(block // LANES):
        here = slice(j * LANES, (j + 1) * LANES)
        out = jnp.zeros((8, LANES), F32)
        for c in range(count):
            source = table_ref[:, c * LANES : (c + 1) * LANES]
            taken = jnp.take_along_axis(source, lane[:, here], axis=1, mode="promise_in_bounds")
            out = jnp.where(tile[:, here] == c, taken, out)
        pieces.append(out)
    return jnp.concatenate(pieces, axis=1)


def compact_row(raw, nodes, slots):
    me = lax.axis_index("dom")
    slot = jnp.maximum(raw - nodes, 0)
    off = slot // slots - me
    near = jnp.clip(jnp.where(off < 0, off + REACH, off + REACH - 1), 0, NEAR - 1)
    return jnp.where(raw >= nodes, nodes + near * slots + slot % slots, raw)


def neighbours(parts):
    me = lax.axis_index("dom")
    out = []
    for off in OFFSETS:
        there = me + off
        inside = (there >= 0) & (there < parts)
        out.append((inside, lax.rem(there + parts, parts)))
    return out


def remote(src, dst, send_sem, recv_sem, partner):
    return pltpu.make_async_remote_copy(
        src_ref=src,
        dst_ref=dst,
        send_sem=send_sem,
        recv_sem=recv_sem,
        device_id={"dom": partner},
        device_id_type=pl.DeviceIdType.MESH,
    )


def start_kernel(
    parts,
    lat_ref,
    pos_ref,
    cen_ref,
    amp_ref,
    rows_ref,
    halo_ref,
    place_ref,
    phi_ref,
    out_s,
    pout_s,
    pin_s,
    base_s,
    cmat_s,
    phi_s,
    send_sem,
    recv_sem,
    psend_sem,
    precv_sem,
    phi_sem,
):
    nodes = lat_ref.shape[0]
    slots = rows_ref.shape[2]
    controls = cen_ref.shape[1]
    partners = neighbours(parts)
    barrier = pltpu.get_barrier_semaphore()
    for inside, partner in partners:

        @pl.when(inside)
        def _():
            pl.semaphore_signal(
                barrier, inc=1, device_id={"dom": partner}, device_id_type=pl.DeviceIdType.MESH
            )

    rows = [rows_ref[0, pl.ds(partner, 1), :] for _, partner in partners]
    base_s[...] = stack_rows([pos_ref[k : k + 1, :] for k in range(3)], 8)
    match = columns_match(jnp.concatenate(rows, axis=1), nodes)
    taken = dot(match, lat_ref[...]).astype(BF16)
    for k in range(NEAR):
        out_s[k] = taken[k * slots : (k + 1) * slots]
        pout_s[k] = lane_gather(base_s, rows[k], nodes // LANES)
    for k, (inside, _) in enumerate(partners):

        @pl.when(jnp.logical_not(inside))
        def _():
            halo_ref[k] = jnp.zeros_like(halo_ref[k])
            pin_s[k] = jnp.zeros_like(pin_s[k])

    def copies(k):
        there = NEAR - 1 - k
        partner = partners[k][1]
        return (
            remote(out_s.at[k], halo_ref.at[there], send_sem.at[k], recv_sem.at[there], partner),
            remote(pout_s.at[k], pin_s.at[there], psend_sem.at[k], precv_sem.at[there], partner),
        )

    pl.semaphore_wait(barrier, sum(inside.astype(jnp.int32) for inside, _ in partners))

    for k, (inside, _) in enumerate(partners):

        @pl.when(inside)
        def _():
            for copy in copies(k):
                copy.start()

    cen = [SCALE * (cen_ref[k : k + 1, :] - 0.5) for k in range(3)]
    crows = []
    for k in range(3):
        hi, mid, low = three(cen[k])
        crows += [hi, mid, hi, low, mid, hi]
    ones = jnp.ones_like(cen[0])
    crows += [ones, ones, ones]
    crows += list(three(-(cen[0] * cen[0] + cen[1] * cen[1] + cen[2] * cen[2])))
    cmat_s[...] = jnp.concatenate(
        [stack_rows(crows[j : j + 8], 8) for j in range(0, 24, 8)]
        + [jnp.zeros((LANES - 24, controls), F32)],
        axis=0,
    ).astype(BF16)
    amp = stack_rows([amp_ref[k : k + 1, :] for k in range(3)], 8)
    amp_hi = amp.astype(BF16).astype(F32)
    amp16 = jnp.concatenate([amp_hi, amp - amp_hi], axis=0).astype(BF16)

    def radial(base, first, size, index):
        moved = jnp.clip(SCALE * (base - 0.5), -FAR, FAR)
        parts_of = [three(moved[k : k + 1]) for k in range(3)]
        prows = []
        for hi, mid, low in parts_of:
            hi2, mid2, low2 = 2.0 * hi, 2.0 * mid, 2.0 * low
            prows += [hi2, hi2, mid2, hi2, mid2, low2]
        norm = moved[0:1] * moved[0:1] + moved[1:2] * moved[1:2] + moved[2:3] * moved[2:3]
        prows += list(three(-norm))
        one = jnp.ones_like(norm)
        prows += [one, one, one]
        wide = jnp.concatenate(
            [stack_rows(prows[j : j + 8], 8) for j in range(0, 24, 8)]
            + [jnp.zeros((LANES - 24, size), F32)],
            axis=0,
        )
        left = jnp.transpose(wide).astype(BF16)
        phi = jnp.exp2(dot(left, cmat_s[...])).astype(BF16)
        phi_s[pl.ds(first, size), :] = phi
        shift = dot_t(amp16, phi)
        place_ref[:, pl.ds(first, size)] = base + (shift[0:8] + shift[8:16])
        pltpu.make_async_copy(
            phi_s.at[pl.ds(first, size)], phi_ref.at[pl.ds(first, size)], phi_sem.at[index]
        ).start()

    size = 256
    own = nodes // size

    def own_step(i, carry):
        first = pl.multiple_of(i * size, size)
        radial(base_s[:, pl.ds(first, size)], first, size, i)
        return carry

    lax.fori_loop(0, own, own_step, 0)
    for k, (inside, _) in enumerate(partners):

        @pl.when(inside)
        def _():
            for copy in copies(NEAR - 1 - k):
                copy.wait_recv()

    pair = size // slots
    for j in range(NEAR // pair):
        halo = jnp.concatenate([pin_s[j * pair + i] for i in range(pair)], axis=1)
        radial(halo, nodes + j * size, size, own + j)
    for k, (inside, _) in enumerate(partners):

        @pl.when(inside)
        def _():
            for copy in copies(k):
                copy.wait_send()

    for i in range(own + NEAR // pair):
        here = pl.ds(i * size, size)
        pltpu.make_async_copy(phi_s.at[here], phi_ref.at[here], phi_sem.at[i]).wait()


def start(node_latent, base_pos, centers, amplitudes, send_rows, parts):
    nodes, width = node_latent.shape
    slots = send_rows.shape[2]
    controls = centers.shape[1]
    every = nodes + NEAR * slots
    return pl.pallas_call(
        functools.partial(start_kernel, parts),
        in_specs=[VMEM_FULL] * 5,
        out_specs=[VMEM_FULL, VMEM_FULL, ANY],
        out_shape=[
            jax.ShapeDtypeStruct((NEAR, slots, width), BF16),
            jax.ShapeDtypeStruct((8, every), F32),
            jax.ShapeDtypeStruct((every, controls), BF16),
        ],
        scratch_shapes=[
            pltpu.VMEM((NEAR, slots, width), BF16),
            pltpu.VMEM((NEAR, 8, slots), F32),
            pltpu.VMEM((NEAR, 8, slots), F32),
            pltpu.VMEM((8, nodes), F32),
            pltpu.VMEM((LANES, controls), BF16),
            pltpu.VMEM((every, controls), BF16),
            pltpu.SemaphoreType.DMA((NEAR,)),
            pltpu.SemaphoreType.DMA((NEAR,)),
            pltpu.SemaphoreType.DMA((NEAR,)),
            pltpu.SemaphoreType.DMA((NEAR,)),
            pltpu.SemaphoreType.DMA((every // 256,)),
        ],
        compiler_params=pltpu.CompilerParams(collective_id=0, has_side_effects=True),
        name="start",
    )(node_latent, base_pos, centers, amplitudes, send_rows)


def normed_of(values):
    centred = values - jnp.mean(values, axis=-1, keepdims=True)
    inv = lax.rsqrt(jnp.mean(centred * centred, axis=-1, keepdims=True) + 1e-05)
    return centred * inv, inv


def norm_back(values, gain, upstream):
    normed, inv = normed_of(values)
    scaled = upstream * gain
    return inv * (
        scaled
        - jnp.mean(scaled, axis=-1, keepdims=True)
        - normed * jnp.mean(scaled * normed, axis=-1, keepdims=True)
    )


def sigmoid(values):
    return 0.5 * jnp.tanh(0.5 * values) + 0.5


def paired(values, weights):
    half = values.shape[0] // 2
    out = dot(jnp.concatenate([values[:half], values[half:]], axis=1), weights)
    return jnp.concatenate([out[:, :LANES], out[:, LANES:]], axis=0)


def picked(pair, second):
    pair = pair.astype(BF16)
    return jnp.where(second, pair[:, LANES:], pair[:, :LANES])


def halves(values, second):
    zero = jnp.zeros_like(values)
    return jnp.concatenate([jnp.where(second, zero, values), jnp.where(second, values, zero)], axis=1)


def edges_kernel(
    sidx_ref,
    ridx_ref,
    lat_ref,
    halo_ref,
    place_ref,
    phi_ref,
    elat_ref,
    ecot_ref,
    ncot_ref,
    ein_ref,
    egeo_ref,
    eout_ref,
    egain_ref,
    nin_ref,
    nout_ref,
    ngain_ref,
    gedge_ref,
    ghid_ref,
    gnode_ref,
    ctrl_ref,
    phi_s,
    phi_sem,
    stab_s,
    rtab_s,
    gtab_s,
    win_s,
    wout_s,
    woutt_s,
    wback_s,
    slope_s,
    normed_s,
    rkey_s,
    rtile_s,
    stile_s,
    unit_s,
    agg_s,
    sgeo_s,
    rgeo_s,
):
    phase = pl.program_id(0)
    step = pl.program_id(1)
    last = pl.num_programs(1) - 1
    nodes, width = lat_ref.shape
    away = halo_ref.shape[0]
    every = nodes + away
    slots = away // NEAR
    block = elat_ref.shape[0]
    at = pl.ds(pl.multiple_of(step * block, block), block)
    shalf = every // 2
    rhalf = nodes // 2
    load_phi = pltpu.make_async_copy(phi_ref, phi_s, phi_sem)

    @pl.when((phase == 0) & (step == 0))
    def _():
        load_phi.start()
        agg_s[...] = jnp.zeros_like(agg_s)
        sgeo_s[...] = jnp.zeros_like(sgeo_s)
        rgeo_s[...] = jnp.zeros_like(rgeo_s)
        stab_s[:, :width] = lat_ref[:shalf]
        stab_s[: nodes - shalf, width:] = lat_ref[shalf:]
        stab_s[nodes - shalf :, width:] = halo_ref[...]
        rtab_s[:, :width] = lat_ref[:rhalf]
        rtab_s[:, width:] = lat_ref[rhalf:]
        geo = stack_rows([egeo_ref[k : k + 1, :] for k in range(4)], 8)
        hi = geo.astype(BF16).astype(F32)
        win_s[: 3 * width] = ein_ref[...]
        win_s[3 * width :] = jnp.concatenate(
            [hi + pltpu.roll(hi, 4, 0), geo - hi, jnp.zeros((LANES - 16, width), F32)], axis=0
        ).astype(BF16)
        w_out = eout_ref[...]
        zero = jnp.zeros_like(w_out)
        turned = jnp.transpose(w_out.astype(F32)).astype(BF16)
        wout_s[...] = jnp.concatenate(
            [jnp.concatenate([w_out, zero], axis=1), jnp.concatenate([zero, w_out], axis=1)], axis=0
        )
        woutt_s[...] = jnp.concatenate(
            [jnp.concatenate([turned, zero], axis=1), jnp.concatenate([zero, turned], axis=1)],
            axis=0,
        )
        w_edge = jnp.transpose(ein_ref[2 * width :].astype(F32)).astype(BF16)
        third = egeo_ref[3:4, :]
        spread = stack_rows(
            [egeo_ref[k : k + 1, :] for k in range(3)] + [None, third, third, third], 8
        )
        spread = jnp.transpose(jnp.concatenate([spread] * (LANES // 8), axis=0)).astype(BF16)
        wback_s[...] = jnp.concatenate(
            [
                jnp.concatenate([w_edge, spread], axis=1),
                jnp.concatenate([zero, spread], axis=1),
            ],
            axis=0,
        )

    @pl.when(phase == 0)
    def _():
        srow = compact_row(sidx_ref[0], nodes, slots)
        rrow = ridx_ref[0]
        delta = lane_gather(place_ref, srow, every // LANES) - lane_gather(
            place_ref, rrow, nodes // LANES
        )
        length = jnp.sqrt(jnp.sum(delta * delta, axis=0, keepdims=True) + 0.01)
        level = lax.broadcasted_iota(jnp.int32, delta.shape, 0)
        geo = jnp.where(level == 3, length, delta)
        hi = geo.astype(BF16).astype(F32)
        wide = jnp.concatenate(
            [hi + pltpu.roll(geo - hi, 4, 0), hi, jnp.zeros((LANES - 16, block), F32)], axis=0
        ).astype(BF16)
        geo_cols = jnp.transpose(wide)
        unit = jnp.where(level < 3, 1.0, pltpu.roll(delta * (1.0 / length), 4, 0)).astype(F32)
        unit_s[at, :] = jnp.transpose(
            jnp.concatenate([unit] * (LANES // 8), axis=0).astype(BF16)
        )

        lane = lane_iota((block, LANES))
        none = jnp.full_like(lane, -1.0)
        stile = as_columns(srow // LANES)
        second = stile >= jnp.full_like(stile, shalf // LANES)
        local = jnp.where(second, stile - jnp.full_like(stile, shalf // LANES), stile)
        skey = jnp.where(as_columns(srow % LANES) == lane, local, none)
        sent = picked(dot(tiles_match(skey, shalf // LANES), stab_s[...]), second)
        rtile = as_columns(rrow // LANES)
        upper = rtile >= jnp.full_like(rtile, rhalf // LANES)
        local = jnp.where(upper, rtile - jnp.full_like(rtile, rhalf // LANES), rtile)
        rkey = jnp.where(as_columns(rrow % LANES) == lane, local, none)
        got = picked(dot(tiles_match(rkey, rhalf // LANES), rtab_s[...]), upper)
        stile_s[at, :] = stile
        rtile_s[at, :] = rtile
        rkey_s[at, :] = rkey

        latent = elat_ref[...]
        pre = dot(jnp.concatenate([sent, got, latent, geo_cols], axis=1), win_s[...])
        sigma = sigmoid(pre)
        hidden = pre * sigma
        slope = sigma + hidden * (1.0 - sigma)
        normed, inv = normed_of(paired(hidden.astype(BF16), wout_s[...]))
        slope_s[at, :] = slope * inv
        normed_s[at, :] = normed
        updated = (latent.astype(F32) + normed * egain_ref[...]).astype(BF16)
        agg_s[...] += dot(rows_match(rrow % rhalf, rhalf), halves(updated, upper))

    @pl.when((phase == 0) & (step == last))
    def _():
        latent = lat_ref[...]
        w_node = nin_ref[:width, :]
        w_agg = nin_ref[width:, :]
        cot = ncot_ref[...].astype(F32)
        agg = jnp.concatenate([agg_s[:, :width], agg_s[:, width:]], axis=0).astype(BF16)
        node_pre = dot(jnp.concatenate([latent, agg], axis=1), nin_ref[...])
        sigma = sigmoid(node_pre)
        hidden = node_pre * sigma
        node_mid = dot(hidden.astype(BF16), nout_ref[...])
        grad_mid = norm_back(node_mid, ngain_ref[...], cot).astype(BF16)
        grad_pre = (
            dot_t(grad_mid, nout_ref[...]) * (sigma + hidden * (1.0 - sigma))
        ).astype(BF16)
        gagg = dot_t(grad_pre, w_agg).astype(BF16)
        gtab_s[...] = jnp.concatenate([gagg[:rhalf], gagg[rhalf:]], axis=1)
        gnode_ref[...] = cot + dot_t(grad_pre, w_node)

    @pl.when(phase == 1)
    def _():
        rtile = rtile_s[at, :]
        stile = stile_s[at, :]
        normed = normed_s[at, :]
        upper = rtile >= jnp.full_like(rtile, rhalf // LANES)
        spread = picked(dot(tiles_match(rkey_s[at, :], rhalf // LANES), gtab_s[...]), upper)
        grad_upd = ecot_ref[...].astype(F32) + spread.astype(F32)
        scaled = grad_upd * egain_ref[...]
        inner = (
            scaled
            - jnp.mean(scaled, axis=-1, keepdims=True)
            - normed * jnp.mean(scaled * normed, axis=-1, keepdims=True)
        )
        grad_pre = paired(inner.astype(BF16), woutt_s[...]) * slope_s[at, :]
        hi, lo = split(grad_pre)
        ghid_ref[...] = hi
        back = dot(jnp.concatenate([hi, lo], axis=1), wback_s[...])
        gedge_ref[...] = grad_upd + back[:, :width]
        moved = (back[:, width:] * unit_s[at, :].astype(F32)).astype(BF16)
        holder = (lax.broadcasted_iota(jnp.int32, (block, LANES), 1) // 8).astype(F32).astype(BF16)
        zero = jnp.zeros_like(moved)
        srow = compact_row(sidx_ref[0], nodes, slots)
        rrow = ridx_ref[0]
        sgeo_s[...] += dot(rows_match(srow % LANES, LANES), jnp.where(holder == stile, moved, zero))
        rgeo_s[...] += dot(rows_match(rrow % LANES, LANES), jnp.where(holder == rtile, moved, zero))

    @pl.when((phase == 1) & (step == last))
    def _():
        load_phi.wait()
        sgeo = jnp.transpose(sgeo_s[...])
        rgeo = jnp.transpose(rgeo_s[...])
        tiles = []
        for t in range(every // LANES):
            tile = sgeo[8 * t : 8 * t + 8]
            if t < nodes // LANES:
                tile = tile - rgeo[8 * t : 8 * t + 8]
            tiles.append(tile + pltpu.roll(tile, 4, 0))
        gpos = jnp.concatenate(tiles, axis=1)
        gpos = jnp.where(lax.broadcasted_iota(jnp.int32, gpos.shape, 0) < 3, gpos, 0.0)
        hi = gpos.astype(BF16).astype(F32)
        both = jnp.concatenate([hi, gpos - hi], axis=0).astype(BF16)
        amp = dot(both, phi_s[...])
        amp = amp[0:8] + amp[8:16]
        for j in range(ctrl_ref.shape[0]):
            ctrl_ref[j] = amp[0:4, j * LANES : (j + 1) * LANES]


def edges(senders, receivers, lat, halo, place, phi, edge_latent, edge_cot, node_cot, weights):
    count, width = edge_latent.shape
    block = 1024 if count % 1024 == 0 else 512
    turns = count // block
    nodes = lat.shape[0]
    away = halo.shape[0]
    every = nodes + away
    controls = phi.shape[1]
    full = lambda shape: pl.BlockSpec(shape, lambda p, i: (0,) * len(shape))
    index_spec = pl.BlockSpec((1, 1, block), lambda p, i: (i, 0, 0))
    second = pl.BlockSpec((block, width), lambda p, i: (i * p, 0))
    chunks = (controls // LANES, 4, LANES)
    return pl.pallas_call(
        edges_kernel,
        grid=(2, turns),
        in_specs=[
            index_spec,
            index_spec,
            full(lat.shape),
            full(halo.shape),
            full(place.shape),
            ANY,
            pl.BlockSpec((block, width), lambda p, i: (i * (1 - p), 0)),
            second,
            full(node_cot.shape),
        ]
        + [full(w.shape) for w in weights],
        out_specs=[second, second, full((nodes, width)), full(chunks)],
        out_shape=[
            jax.ShapeDtypeStruct((count, width), F32),
            jax.ShapeDtypeStruct((count, width), BF16),
            jax.ShapeDtypeStruct((nodes, width), F32),
            jax.ShapeDtypeStruct(chunks, F32),
        ],
        scratch_shapes=[
            pltpu.VMEM((every, controls), BF16),
            pltpu.SemaphoreType.DMA,
            pltpu.VMEM((every // 2, 2 * width), BF16),
            pltpu.VMEM((nodes // 2, 2 * width), BF16),
            pltpu.VMEM((nodes // 2, 2 * width), BF16),
            pltpu.VMEM((3 * width + LANES, width), BF16),
            pltpu.VMEM((2 * width, 2 * width), BF16),
            pltpu.VMEM((2 * width, 2 * width), BF16),
            pltpu.VMEM((2 * width, width + LANES), BF16),
            pltpu.VMEM((count, width), F32),
            pltpu.VMEM((count, width), F32),
            pltpu.VMEM((count, LANES), BF16),
            pltpu.VMEM((count, LANES), BF16),
            pltpu.VMEM((count, LANES), BF16),
            pltpu.VMEM((count, LANES), BF16),
            pltpu.VMEM((nodes // 2, 2 * width), F32),
            pltpu.VMEM((LANES, LANES), F32),
            pltpu.VMEM((LANES, LANES), F32),
        ],
        compiler_params=pltpu.CompilerParams(
            dimension_semantics=("arbitrary", "arbitrary")
        ),
        name="edges",
    )(
        senders.reshape(turns, 1, block),
        receivers.reshape(turns, 1, block),
        lat,
        halo,
        place,
        phi,
        edge_latent,
        edge_cot,
        node_cot,
        *weights,
    )


def tail_kernel(
    parts,
    sidx_ref,
    ridx_ref,
    ghid_ref,
    gnode_ref,
    ctrl_ref,
    rows_ref,
    ein_ref,
    out_ref,
    amp_ref,
    sum_s,
    rsum_s,
    back_s,
    got_s,
    part_s,
    mine_s,
    all_s,
    back_send,
    back_recv,
    part_send,
    part_recv,
    all_send,
    all_recv,
):
    me = lax.axis_index("dom")
    turns, _, block = sidx_ref.shape
    nodes, width = gnode_ref.shape
    slots = rows_ref.shape[2]
    every = nodes + NEAR * slots
    shalf = every // 2
    rhalf = nodes // 2
    chunks = ctrl_ref.shape[0]
    reducers = max(r for r in range(1, parts + 1) if chunks % r == 0)
    per = chunks // reducers
    partners = neighbours(parts)
    others = [lax.rem(me + i, parts) for i in range(1, parts)]
    sources = [lax.rem(me + parts - i, parts) for i in range(1, parts)]
    barrier = pltpu.get_barrier_semaphore()
    for other in others:
        pl.semaphore_signal(
            barrier, inc=1, device_id={"dom": other}, device_id_type=pl.DeviceIdType.MESH
        )
    sum_s[...] = jnp.zeros_like(sum_s)
    rsum_s[...] = jnp.zeros_like(rsum_s)
    for k, (inside, _) in enumerate(partners):

        @pl.when(jnp.logical_not(inside))
        def _():
            got_s[k] = jnp.zeros_like(got_s[k])

    pl.semaphore_wait(barrier, parts - 1)

    def part_copy(i):
        other = others[i]
        return remote(
            ctrl_ref.at[pl.ds(jnp.minimum(other, reducers - 1) * per, per)],
            part_s.at[i],
            part_send.at[i],
            part_recv.at[i],
            other,
        )

    def all_copy(i):
        return remote(
            mine_s,
            all_s.at[pl.ds(jnp.minimum(me, reducers - 1) * per, per)],
            all_send.at[i],
            all_recv.at[i],
            others[i],
        )

    def when_reducer(device, run):
        if reducers == parts:
            run()
        else:
            pl.when(device < reducers)(run)

    for i in range(parts - 1):
        when_reducer(others[i], lambda: part_copy(i).start())

    def sender_step(t, carry):
        srow = compact_row(sidx_ref[t], nodes, slots)
        stile = as_columns(srow // LANES)
        second = stile >= jnp.full_like(stile, shalf // LANES)
        values = ghid_ref[pl.ds(pl.multiple_of(t * block, block), block), :]
        sum_s[...] += dot(rows_match(srow % shalf, shalf), halves(values, second))
        return carry

    lax.fori_loop(0, turns, sender_step, 0)
    w_send = ein_ref[:width]
    w_recv = ein_ref[width : 2 * width]

    def projected(values, weight):
        hi, lo = split(values)
        return dot_t(hi, weight) + dot_t(lo, weight)

    back = projected(sum_s[shalf - NEAR * slots :, width:], w_send).astype(BF16)
    for k in range(NEAR):
        back_s[k] = back[k * slots : (k + 1) * slots]

    def back_copy(k):
        there = NEAR - 1 - k
        return remote(
            back_s.at[k], got_s.at[there], back_send.at[k], back_recv.at[there], partners[k][1]
        )

    def reduce_mine():
        total = ctrl_ref[pl.ds(jnp.minimum(me, reducers - 1) * per, per)]
        for i in range(parts - 1):
            part_copy(i).wait_recv()
        for i in range(parts - 1):
            total = total + part_s[i]
        mine_s[...] = total
        all_s[pl.ds(jnp.minimum(me, reducers - 1) * per, per)] = total

    when_reducer(me, reduce_mine)
    for k, (inside, _) in enumerate(partners):

        @pl.when(inside)
        def _():
            back_copy(k).start()

    def send_all():
        for i in range(parts - 1):
            all_copy(i).start()

    when_reducer(me, send_all)

    def receiver_step(t, carry):
        rrow = ridx_ref[t]
        rtile = as_columns(rrow // LANES)
        upper = rtile >= jnp.full_like(rtile, rhalf // LANES)
        values = ghid_ref[pl.ds(pl.multiple_of(t * block, block), block), :]
        rsum_s[...] += dot(rows_match(rrow % rhalf, rhalf), halves(values, upper))
        return carry

    lax.fori_loop(0, turns, receiver_step, 0)
    sent = jnp.concatenate([sum_s[:, :width], sum_s[: nodes - shalf, width:]], axis=0)
    received = jnp.concatenate([rsum_s[:, :width], rsum_s[:, width:]], axis=0)
    total = gnode_ref[...] + projected(sent, w_send) + projected(received, w_recv)
    for k, (inside, _) in enumerate(partners):

        @pl.when(inside)
        def _():
            back_copy(NEAR - 1 - k).wait_recv()

    rows = jnp.concatenate([rows_ref[0, pl.ds(partner, 1), :] for _, partner in partners], axis=1)
    got = jnp.concatenate([got_s[k] for k in range(NEAR)], axis=0)
    out_ref[...] = total + dot(rows_match(rows, nodes), got)
    for k, (inside, _) in enumerate(partners):

        @pl.when(inside)
        def _():
            back_copy(k).wait_send()

    for i in range(parts - 1):
        when_reducer(others[i], lambda: part_copy(i).wait_send())
    when_reducer(me, lambda: [all_copy(i).wait_send() for i in range(parts - 1)] and None)
    for i in range(parts - 1):
        source = sources[i]

        def arrived():
            remote(
                mine_s,
                all_s.at[pl.ds(jnp.minimum(source, reducers - 1) * per, per)],
                all_send.at[i],
                all_recv.at[i],
                others[i],
            ).wait_recv()

        when_reducer(source, arrived)
    for j in range(chunks):
        amp_ref[:, j * LANES : (j + 1) * LANES] = all_s[j][0:3]


def tail(senders, receivers, ghid, gnode, ctrl, send_rows, edge_in, parts):
    count, width = ghid.shape
    block = 1024 if count % 1024 == 0 else 512
    turns = count // block
    nodes = gnode.shape[0]
    slots = send_rows.shape[2]
    every = nodes + NEAR * slots
    chunks = ctrl.shape[0]
    reducers = max(r for r in range(1, parts + 1) if chunks % r == 0)
    per = (chunks // reducers,) + ctrl.shape[1:]
    sems = pltpu.SemaphoreType.DMA((parts - 1,))
    return pl.pallas_call(
        functools.partial(tail_kernel, parts),
        in_specs=[VMEM_FULL] * 7,
        out_specs=[VMEM_FULL, VMEM_FULL],
        out_shape=[
            jax.ShapeDtypeStruct(gnode.shape, F32),
            jax.ShapeDtypeStruct((3, chunks * LANES), F32),
        ],
        scratch_shapes=[
            pltpu.VMEM((every // 2, 2 * width), F32),
            pltpu.VMEM((nodes // 2, 2 * width), F32),
            pltpu.VMEM((NEAR, slots, width), BF16),
            pltpu.VMEM((NEAR, slots, width), BF16),
            pltpu.VMEM((parts - 1,) + per, F32),
            pltpu.VMEM(per, F32),
            pltpu.VMEM(ctrl.shape, F32),
            pltpu.SemaphoreType.DMA((NEAR,)),
            pltpu.SemaphoreType.DMA((NEAR,)),
            sems,
            sems,
            sems,
            sems,
        ],
        compiler_params=pltpu.CompilerParams(collective_id=1, has_side_effects=True),
        name="tail",
    )(
        senders.reshape(turns, 1, block),
        receivers.reshape(turns, 1, block),
        ghid,
        gnode,
        ctrl,
        send_rows,
        edge_in,
    )


def shards(
    node_latent,
    edge_latent,
    node_cot,
    edge_cot,
    base_pos,
    centers,
    amplitudes,
    edge_in,
    edge_geo,
    edge_out,
    edge_gain,
    node_in,
    node_out,
    node_gain,
    senders,
    receivers,
    send_rows,
):
    parts = lax.axis_size("dom")
    width = node_latent.shape[1]
    halo, place, phi = start(node_latent, base_pos, centers, amplitudes, send_rows, parts)
    weights = (
        edge_in,
        edge_geo,
        edge_out,
        edge_gain[None, :],
        node_in,
        node_out,
        node_gain[None, :],
    )
    grad_edges, ghid, gnode, ctrl = edges(
        senders,
        receivers,
        node_latent,
        halo.reshape(-1, width),
        place,
        phi,
        edge_latent,
        edge_cot,
        node_cot,
        weights,
    )
    grad_nodes, grad_controls = tail(
        senders, receivers, ghid, gnode, ctrl, send_rows, edge_in, parts
    )
    return (grad_nodes, grad_edges, grad_controls)


def solution(mesh):
    split_rows = P(("groups", "dom"), None)
    in_specs = (
        split_rows,
        split_rows,
        split_rows,
        split_rows,
        P(None, ("groups", "dom")),
        P(),
        P(),
        P(),
        P(),
        P(),
        P(),
        P(),
        P(),
        P(),
        P(("groups", "dom")),
        P(("groups", "dom")),
        P(("groups", "dom"), None, None),
    )
    out_specs = (split_rows, split_rows, P("groups", None))
    return jax.shard_map(shards, mesh=mesh, in_specs=in_specs, out_specs=out_specs, check_vma=False)
```

time: 112 us -> 60.2 us (0.54)
  Pallas kernels: 106 us -> 56 us
  other arithmetic: 2.7 us -> 0 us
  local copies, waits for them, and re-layouts: 1.47 us -> 3.25 us
    pallas_call x1, Pallas kernels: 54.8 us -> 29.6 us  [edges(): pl.pallas_call(edges_kernel, grid=(2, turns), in_specs=[index_spec, index...]
    pallas_call x5 -> x2, Pallas kernels: 51.6 us -> 26.4 us  [the longest x1 15.5 us: tail(): pl.pallas_call(functools.partial(tail_kernel, parts), in_specs=[VMEM_FULL...]
    unnamed x0 -> x2, local copies, waits for them, and re-layouts: none -> 3.25 us
    slice x2 -> x0, local copies, waits for them, and re-layouts: 1.47 us -> none  [the longest x1 1.46 us: shards(): grad_controls = total(amp, parts, 2)[:3]]
    select_n x1 -> x0, other arithmetic: 1.38 us -> none  [shards(): jnp.where(senders >= nodes, nodes + near * slots + slot % slots, senders)]
    concatenate x2 -> x0, other arithmetic: 1.31 us -> none  [the longest x1 0.72 us: shards(): twice = jnp.concatenate([send_rows[0], send_rows[0]], 0)]
where the time goes in v1:
time: 60.2 us; the launch traced here: 59.9 us
  Pallas kernels  56 us (93%)
  local copies, waits for them, and re-layouts  3.25 us (5%)
  between operations  0.66 us (1%)
    pallas_call x1, Pallas kernels, edges(): pl.pallas_call(edges_kernel, grid=(2, turns), in_specs=[index_spec, index...  29.6 us
    pallas_call x1, Pallas kernels, tail(): pl.pallas_call(functools.partial(tail_kernel, parts), in_specs=[VMEM_FULL...  15.5 us
    pallas_call x1, Pallas kernels, start(): pl.pallas_call(functools.partial(start_kernel, parts), in_specs=[VMEM_FUL...  10.9 us
    unnamed x2, local copies, waits for them, and re-layouts  3.25 us

profile of v1, /device:TPU:0, one launch (start us, length us, event | category | flops | bytes accessed | tf_op | source)
XLA Modules:
  0.0 59.9 jit_solution(14326313682006803244)
XLA Ops:
  0.6 10.9 %start.1 = (bf16[4,128,128]{2,1,0:T(8,128)(2,1)}, f32[8,1536]{1,0:T(8,128)}, bf16[1536,2048]{1,0:T(8,128)(2,1)}) custom-call(bf16[1024,128]{1,0:T(8,128)(2,1)} %lat_ref.3, f32[3,1024]{1,0:T(4,128)} %pos_ref.1, f32[3,2048]{1,0:T(4,128)} %cen_ref.1, f32[3,2048]{1,0:T(4,128)} %amp_ref.1, s32[1,16,128]{2,1,0:T(8,128)} %rows_ref.3), custom_call_target="tpu_custom_call" | custom-call | tf_op jit(solution)/shard_map/start/pallas_call | solution.py:276
  11.6 29.6 %edges.1 = (f32[6144,128]{1,0:T(8,128)}, bf16[6144,128]{1,0:T(8,128)(2,1)}, f32[1024,128]{1,0:T(8,128)}, f32[16,4,128]{2,1,0:T(4,128)}) custom-call(s32[6,1,1024]{2,1,0:T(1,128)} %bitcast.6, s32[6,1,1024]{2,1,0:T(1,128)} %bitcast.8, bf16[1024,128]{1,0:T(8,128)(2,1)} %lat_ref.3, bf16[512,128]{1,0:T(8,128)(2,1)} %bitcast.5, ...), custom_call_target="tpu_custom_call" | custom-call | tf_op jit(solution)/shard_map/edges/pallas_call | solution.py:559
  41.2 15.5 %tail.1 = (f32[1024,128]{1,0:T(8,128)}, f32[3,2048]{1,0:T(4,128)}) custom-call(s32[6,1,1024]{2,1,0:T(1,128)} %bitcast.7, s32[6,1,1024]{2,1,0:T(1,128)} %bitcast.9, bf16[6144,128]{1,0:T(8,128)(2,1)} %get-tuple-element.15.ghid_ref, f32[1024,128]{1,0:T(8,128)} %get-tuple-element.16.gnode_ref, f32[16,4,128]{2,1,0:T(4,128)} %get-tuple-element.17.ctrl_ref, ...), custom_call_target="tpu_custom_call" | custom-call | tf_op jit(solution)/shard_map/tail/pallas_call | solution.py:806
  56.7 1.9 %copy.22 = f32[1024,128]{1,0:T(8,128)} copy(f32[1024,128]{1,0:T(8,128)} %get-tuple-element.24) | data formatting | bytes 1048576
  58.5 1.4 %copy.23 = f32[3,2048]{1,0:T(4,128)} copy(f32[3,2048]{1,0:T(4,128)} %get-tuple-element.26) | data formatting | bytes 49152
